TPU v7x, 32 devices: a whole 2x2x4 slice. The times are simulated.
32 devices in a mesh: rows: 8 (over z, y), grp: 4 (over x, core).
Axes of the slice: x: 2, y: 2, z: 4, core: 2. Of those that a mesh axis runs over, the one named last changes fastest.
Arguments:
- table: float32 [65536, 256], P(('rows', 'grp')), may hold values from -1.5 to 1.5
- hot_slot: int32 [512], P(('rows', 'grp')), may hold values from 0 to 2047, as said below
- cold_row: int32 [32, 32, 64], P(('rows', 'grp')), may hold values from 0 to 2047, as said below
- cold_bag: int32 [32, 32, 64], P(('rows', 'grp')), may hold values from 0 to 511
- hot_pick: int32 [8192, 8], P(('rows', 'grp')), may hold values from 0 to 511
- dense: float32 [8192, 256], P(('rows', 'grp')), may hold values from -6 to 6
- label: int32 [8192], P(('rows', 'grp')), may hold values 0 or 1
Outputs:
- pooled: float32 [8192, 256], P(('rows', 'grp'))
- new_table: float32 [65536, 256], P(('rows', 'grp'))
- hot_new: float32 [512, 256], replicated
Inputs may be any that keep to these rules, and one draw needn't show every extreme that they name: `hot_slot`: distinct within each device's block of 16 entries; hot row h lies in the shard of device h // 16. `cold_row`: a cold slot never names a hot row of its owner. `cold_bag`: a value of 256 or more marks an empty slot.
All inputs are finite; a program needn't handle non-finite values. No bound on the sum of `label` on one device may be relied on, other than what follows from the above.
Results may differ from a plain program's by a relative error of at most 0.0029.
Values may be sent and summed in bfloat16 or wider, within the bound.
No kernel may reach another device: no remote copies, remote signals or barrier semaphores. Data moves between devices by JAX's collectives and lax.ppermute only.
A program may use at most 64 MiB of HBM per device.

v0:
```python
import jax
import jax.numpy as jnp
from jax import lax
from jax.sharding import PartitionSpec as P


def body(table, hot_slot, cold_row, cold_bag, hot_pick, dense, label):
    n_rows = lax.axis_size("rows")
    n_grp = lax.axis_size("grp")
    width = table.shape[1]
    samples = dense.shape[0]
    own_hot = hot_slot.shape[0]
    slots = cold_row.shape[1] * cold_row.shape[2]
    per_peer = cold_row.shape[2]
    rounded = table.astype(jnp.bfloat16)
    hot_full = lax.all_gather(table[hot_slot], ("rows", "grp"), axis=0, tiled=True)
    hot_copy = hot_full.astype(jnp.bfloat16)
    requests = cold_row[0].reshape(n_rows, n_grp, per_peer)
    arrived = lax.all_to_all(
        lax.all_to_all(requests, "rows", split_axis=0, concat_axis=0, tiled=True),
        "grp",
        split_axis=1,
        concat_axis=1,
        tiled=True,
    )
    looked = rounded[arrived.reshape(-1)].reshape(n_rows, n_grp, per_peer, width)
    returned = lax.all_to_all(
        lax.all_to_all(looked, "rows", split_axis=0, concat_axis=0, tiled=True),
        "grp",
        split_axis=1,
        concat_axis=1,
        tiled=True,
    )
    flat_rows = returned.reshape(slots, width)
    bags = cold_bag[0].reshape(slots)
    selector = jnp.arange(samples, dtype=jnp.int32)[:, None] == bags[None, :]
    cold_pooled = jnp.dot(
        selector.astype(jnp.bfloat16), flat_rows, preferred_element_type=jnp.float32
    )
    hot_pooled = jnp.sum(hot_copy[hot_pick].astype(jnp.float32), axis=1)
    pooled = cold_pooled + hot_pooled
    score = jnp.sum(pooled * dense, axis=1) / width**0.5
    err = jax.nn.sigmoid(score) - label.astype(jnp.float32)
    grad = err[:, None] * dense
    slot_grad = lax.dot_general(
        selector.astype(jnp.float32),
        grad,
        (((0,), (0,)), ((), ())),
        precision=lax.Precision.HIGHEST,
        preferred_element_type=jnp.float32,
    )
    delivered = lax.all_to_all(
        lax.all_to_all(
            slot_grad.reshape(n_rows, n_grp, per_peer, width),
            "rows",
            split_axis=0,
            concat_axis=0,
            tiled=True,
        ),
        "grp",
        split_axis=1,
        concat_axis=1,
        tiled=True,
    )
    table_grad = jax.ops.segment_sum(
        delivered.reshape(slots, width), arrived.reshape(slots), num_segments=table.shape[0]
    )
    hot_total = hot_copy.shape[0]
    spread = jnp.repeat(grad, hot_pick.shape[1], axis=0)
    hot_local = jax.ops.segment_sum(spread, hot_pick.reshape(-1), num_segments=hot_total)
    quarter = lax.psum_scatter(hot_local, "grp", scatter_dimension=0, tiled=True)
    crossed = lax.psum(quarter, "rows")
    summed = lax.all_gather(crossed, "grp", axis=0, tiled=True)
    start = lax.axis_index(("rows", "grp")) * own_hot
    own_grad = lax.dynamic_slice_in_dim(summed, start, own_hot, 0)
    table_grad = table_grad.at[hot_slot].add(own_grad)
    new_table = table - 0.1 * table_grad
    hot_new = hot_full - 0.1 * summed
    return (pooled, new_table, hot_new)


def solution(mesh):
    placed = (
        P(("rows", "grp"), None),
        P(("rows", "grp")),
        P(("rows", "grp"), None, None),
        P(("rows", "grp"), None, None),
        P(("rows", "grp"), None),
        P(("rows", "grp"), None),
        P(("rows", "grp")),
    )
    return jax.shard_map(
        body,
        mesh=mesh,
        in_specs=placed,
        out_specs=(P(("rows", "grp"), None), P(("rows", "grp"), None), P()),
        check_vma=False,
    )
```

profile of v0, /device:TPU:0, one launch (start us, length us, event | category | flops | bytes accessed | tf_op | source)
XLA Modules:
  0.0 316.5 jit_solution(10149955036070640280)
XLA Ops:
  8.0 13.6 %all_to_all.30 = s32[8,1,256]{2,1,0:T(1,128)S(1)} all-to-all(s32[8,1,256]{2,1,0:T(1,128)S(1)} %reshape.122), channel_id=1, replica_groups=mesh['rows'=8,'grp'=4] {'rows'}, dimensions={0} | all-to-all | bytes 16384 | tf_op jit(solution)/shard_map/all_to_all | solution.py:20
  23.5 3.2 %all-to-all-start.1 = ((s32[4,1,512]{2,1,0:T(1,128)}), s32[4,1,512]{2,1,0:T(1,128)S(1)}, u32[]{:S(2)}, u32[]{:S(2)}) async-start(s32[4,1,512]{2,1,0:T(1,128)} %reshape.124), calls=%async_computation.1 | async-start | bytes 16384 | tf_op jit(solution)/shard_map/all_to_all | solution.py:19
  26.8 1.7 convert_element_type.14
  28.5 2.1 all-to-all-done.1
  31.5 9.1 %gather_fusion = bf16[2048,256]{1,0:T(8,128)(2,1)} fusion(bf16[2048,256]{1,0:T(8,128)(2,1)S(1)} %convert_element_type.14, s32[2048]{0:T(1024)S(1)} %broadcast_clamp_fusion.1), kind=kCustom, calls=%fused_computation | custom fusion | bytes 2105344 | tf_op jit(solution)/shard_map/gather | solution.py:26
  40.5 4.4 %all-to-all-start.2 = ((bf16[8,4,64,256]{3,2,1,0:T(8,128)(2,1)}), bf16[8,4,64,256]{3,2,1,0:T(8,128)(2,1)}, u32[]{:S(2)}, u32[]{:S(2)}) async-start(bf16[8,4,64,256]{3,2,1,0:T(8,128)(2,1)} %bitcast.19), calls=%async_computation.2 | async-start | bytes 2097152 | tf_op jit(solution)/shard_map/all_to_all | solution.py:28
  46.4 24.6 %all-to-all-done.2 = bf16[8,4,64,256]{3,2,1,0:T(8,128)(2,1)} async-done(((bf16[8,4,64,256]{3,2,1,0:T(8,128)(2,1)}), bf16[8,4,64,256]{3,2,1,0:T(8,128)(2,1)}, u32[]{:S(2)}, u32[]{:S(2)}) %all-to-all-start.2) | async-done | bytes 1048608 | tf_op jit(solution)/shard_map/all_to_all | solution.py:28
  70.9 2.3 copy.37
  73.2 4.4 %all-to-all-start.3 = ((bf16[8,4,64,256]{3,2,0,1:T(8,128)(2,1)}), bf16[8,4,64,256]{3,2,0,1:T(8,128)(2,1)}, u32[]{:S(2)}, u32[]{:S(2)}) async-start(bf16[8,4,64,256]{3,2,0,1:T(8,128)(2,1)} %copy.37), calls=%async_computation.3 | async-start | bytes 2097152 | tf_op jit(solution)/shard_map/all_to_all | solution.py:27
  77.6 46.8 %all-gather = f32[512,256]{1,0:T(8,128)S(1)} all-gather(f32[16,256]{1,0:T(8,128)S(1)} %gather_fusion.1), channel_id=2, replica_groups=mesh['rows'=8,'grp'=4] {'rows','grp'}, dimensions={0}, use_global_device_ids=true | all-gather | bytes 540672 | tf_op jit(solution)/shard_map/all_gather | solution.py:16
  124.8 9.1 %gather_fusion.2 = bf16[2048,256]{1,0:T(8,128)(2,1)} fusion(bf16[512,256]{1,0:T(8,128)(2,1)S(1)} %convert_element_type.15, s32[2048]{0:T(1024)S(1)} %broadcast_clamp_fusion), kind=kCustom, calls=%fused_computation.2 | custom fusion | bytes 2105344 | tf_op jit(solution)/shard_map/gather | solution.py:40
  133.8 1.9 convert_reduce_fusion
  139.8 3.2 fusion.2
  142.9 4.3 %all-to-all-start.4 = ((f32[8,4,64,256]{3,2,1,0:T(8,128)}), f32[8,4,64,256]{3,2,1,0:T(8,128)}, u32[]{:S(2)}, u32[]{:S(2)}) async-start(f32[8,4,64,256]{3,2,1,0:T(8,128)} %bitcast.18), calls=%async_computation.4 | async-start | bytes 4194304 | tf_op jit(solution)/shard_map/all_to_all | solution.py:53
  147.6 12.4 %scatter_custom_fusion.1 = f32[512,256]{1,0:T(8,128)} fusion(s32[2048]{0:T(1024)S(1)} %reshape.94, f32[256,256]{1,0:T(8,128)S(1)} %broadcast_multiply_fusion, f32[]{:T(128)} %constant.15.clone.1), kind=kCustom, calls=%fused_computation.7 | custom fusion | flops 524288 | bytes 786436 | tf_op jit(solution)/shard_map/scatter-add | solution.py:70
  160.0 36.3 %all-to-all-done.4 = f32[8,4,64,256]{3,2,1,0:T(8,128)} async-done(((f32[8,4,64,256]{3,2,1,0:T(8,128)}), f32[8,4,64,256]{3,2,1,0:T(8,128)}, u32[]{:S(2)}, u32[]{:S(2)}) %all-to-all-start.4) | async-done | bytes 2097184 | tf_op jit(solution)/shard_map/all_to_all | solution.py:53
  196.3 3.1 copy.43
  199.4 4.4 %all-to-all-start.5 = ((f32[8,4,64,256]{3,2,0,1:T(8,128)}), f32[8,4,64,256]{3,2,0,1:T(8,128)}, u32[]{:S(2)}, u32[]{:S(2)}) async-start(f32[8,4,64,256]{3,2,0,1:T(8,128)} %copy.43), calls=%async_computation.5 | async-start | bytes 4194304 | tf_op jit(solution)/shard_map/all_to_all | solution.py:52
  205.6 72.4 %all-reduce.2.cloned.1.call-done = f32[128,256]{1,0:T(8,128)} async-done(((f32[128,256]{1,0:T(8,128)}), f32[128,256]{1,0:T(8,128)}) %all-reduce.2.cloned.1.call-update) | async-done | bytes 131088 | tf_op jit(solution)/shard_map/psum | solution.py:72
  278.0 7.5 %all_gather.7 = f32[512,256]{1,0:T(8,128)S(1)} all-gather(f32[128,256]{1,0:T(8,128)} %all-reduce.2.cloned.1.call-done), channel_id=1, replica_groups=mesh['rows'=8,'grp'=4] {'grp'}, dimensions={0}, use_global_device_ids=true | all-gather | bytes 655360 | tf_op jit(solution)/shard_map/all_gather | solution.py:73
  286.4 3.1 copy.44
  289.5 13.4 %scatter_custom_fusion = f32[2048,256]{1,0:T(8,128)} fusion(s32[2048]{0:T(1024)S(1)} %reshape.86, f32[2048,256]{1,0:T(8,128)} %bitcast.20, f32[]{:T(128)} %constant.15.clone.1), kind=kCustom, calls=%fused_computation.15 | custom fusion | flops 524288 | bytes 2097664 | tf_op jit(solution)/shard_map/scatter-add | solution.py:65
  302.9 3.6 %scatter_custom_fusion.2 = f32[2048,256]{1,0:T(8,128)} fusion(f32[2048,256]{1,0:T(8,128)} %scatter_custom_fusion, s32[16]{0:T(128)S(1)} %compare_select_fusion.2, f32[512,256]{1,0:T(8,128)S(1)} %all_gather.7, s32[]{:T(128)S(6)} %select_n.23, s32[]{:T(128)} %constant.12.clone.1), kind=kCustom, calls=%fused_computation.25 | custom fusion | flops 4096 | bytes 2114052 | tf_op jit(solution)/shard_map/scatter-add | solution.py:76
  306.5 3.2 %multiply_subtract_fusion = f32[2048,256]{1,0:T(8,128)} fusion(f32[2048,256]{1,0:T(8,128)S(1)} %copy-done, f32[2048,256]{1,0:T(8,128)} %scatter_custom_fusion.2), kind=kLoop, calls=%fused_computation.9 | loop fusion | flops 1048576 | bytes 6291456 | tf_op jit(solution)/shard_map/sub | solution.py:77
  (53 shorter events, 12.1 us)
Async XLA Ops:
  23.5 7.0 %all-to-all-start.1 = ((s32[4,1,512]{2,1,0:T(1,128)}), s32[4,1,512]{2,1,0:T(1,128)S(1)}, u32[]{:S(2)}, u32[]{:S(2)}) async-start(s32[4,1,512]{2,1,0:T(1,128)} %reshape.124), calls=%async_computation.1 | async-start | bytes 16384 | tf_op jit(solution)/shard_map/all_to_all | solution.py:19
  31.5 13.5 %copy-start.1 = (f32[256,256]{1,0:T(8,128)S(1)}, f32[256,256]{1,0:T(8,128)}, u32[]{:S(2)}) copy-start(f32[256,256]{1,0:T(8,128)} %param.12) | copy-start | bytes 786436
  40.5 5.2 %copy-start.6 = (s32[16]{0:T(128)S(1)}, s32[16]{0:T(128)}, u32[]{:S(2)}) copy-start(s32[16]{0:T(128)} %param.8) | copy-start | bytes 196
  40.5 5.2 %copy-start = (f32[2048,256]{1,0:T(8,128)S(1)}, f32[2048,256]{1,0:T(8,128)}, u32[]{:S(2)}) copy-start(f32[2048,256]{1,0:T(8,128)} %param.7) | copy-start | bytes 6291460
  40.5 30.4 %all-to-all-start.2 = ((bf16[8,4,64,256]{3,2,1,0:T(8,128)(2,1)}), bf16[8,4,64,256]{3,2,1,0:T(8,128)(2,1)}, u32[]{:S(2)}, u32[]{:S(2)}) async-start(bf16[8,4,64,256]{3,2,1,0:T(8,128)(2,1)} %bitcast.19), calls=%async_computation.2 | async-start | bytes 2097152 | tf_op jit(solution)/shard_map/all_to_all | solution.py:28
  73.2 51.2 %copy-start.3 = (s32[256,8]{0,1:T(8,128)S(1)}, s32[256,8]{0,1:T(8,128)}, u32[]{:S(2)}) copy-start(s32[256,8]{0,1:T(8,128)} %param.11) | copy-start | bytes 24580
  73.2 63.4 %all-to-all-start.3 = ((bf16[8,4,64,256]{3,2,0,1:T(8,128)(2,1)}), bf16[8,4,64,256]{3,2,0,1:T(8,128)(2,1)}, u32[]{:S(2)}, u32[]{:S(2)}) async-start(bf16[8,4,64,256]{3,2,0,1:T(8,128)(2,1)} %copy.37), calls=%async_computation.3 | async-start | bytes 2097152 | tf_op jit(solution)/shard_map/all_to_all | solution.py:27
  124.7 11.8 %copy-start.4 = (s32[1,32,64]{2,1,0:T(8,128)S(1)}, s32[1,32,64]{2,1,0:T(8,128)}, u32[]{:S(2)}) copy-start(s32[1,32,64]{2,1,0:T(8,128)} %param.10) | copy-start | bytes 24580
  136.6 1.4 copy-start.2
  136.7 3.0 copy-start.5
  142.9 53.4 %all-to-all-start.4 = ((f32[8,4,64,256]{3,2,1,0:T(8,128)}), f32[8,4,64,256]{3,2,1,0:T(8,128)}, u32[]{:S(2)}, u32[]{:S(2)}) async-start(f32[8,4,64,256]{3,2,1,0:T(8,128)} %bitcast.18), calls=%async_computation.4 | async-start | bytes 4194304 | tf_op jit(solution)/shard_map/all_to_all | solution.py:53
  147.3 56.7 %reduce-scatter.2.cloned.1.call-start = ((), (), s32[]{:S(2)}) async-start(), calls=%async_computation.7 | async-start | bytes 655360 | tf_op jit(solution)/shard_map/reduce_scatter | solution.py:71
  199.4 86.9 %all-to-all-start.5 = ((f32[8,4,64,256]{3,2,0,1:T(8,128)}), f32[8,4,64,256]{3,2,0,1:T(8,128)}, u32[]{:S(2)}, u32[]{:S(2)}) async-start(f32[8,4,64,256]{3,2,0,1:T(8,128)} %copy.43), calls=%async_computation.5 | async-start | bytes 4194304 | tf_op jit(solution)/shard_map/all_to_all | solution.py:52
  203.9 74.1 %all-reduce.2.cloned.1.call-start = ((), (), s32[]{:S(2)}) async-start(), calls=%async_computation.8 | async-start | bytes 262144 | tf_op jit(solution)/shard_map/psum | solution.py:72
Sparse Core Ops, SparseCore 0:
  160.1 21.9 reduce-scatter.1
  208.1 69.8 all-reduce.1
where the time goes:
time: 317 us; the launch traced here: 316 us
  waiting for transfers between devices  136 us (43%)
  blocking collectives  67.9 us (21%)
  other arithmetic  38.5 us (12%)
  local copies, waits for them, and re-layouts  34 us (11%)
  starting transfers between devices  20.9 us (7%)
  between operations  14.3 us (5%)
  matrix products  4.82 us (2%)
    psum x1, waiting for transfers between devices, body(): crossed = lax.psum(quarter, 'rows')  72.4 us
    all_gather x1, blocking collectives, body(): lax.all_gather(table[hot_slot], ('rows', 'grp'), axis=0, tiled=True)  46.8 us
    all_to_all x1, waiting for transfers between devices, body(): lax.all_to_all(slot_grad.reshape(n_rows, n_grp, per_peer, width), 'rows',...  36.3 us
    all_to_all x1, waiting for transfers between devices, body(): lax.all_to_all(looked, 'rows', split_axis=0, concat_axis=0, tiled=True)  24.6 us
    all_to_all x1, blocking collectives, body(): lax.all_to_all(requests, 'rows', split_axis=0, concat_axis=0, tiled=True)  13.6 us
    scatter-add x1, other arithmetic, body(): jax.ops.segment_sum(delivered.reshape(slots, width), arrived.reshape(slot...  13.4 us
    scatter-add x1, other arithmetic, body(): jax.ops.segment_sum(spread, hot_pick.reshape(-1), num_segments=hot_total)  12.4 us
    gather x1, local copies, waits for them, and re-layouts, body(): rounded[arrived.reshape(-1)].reshape(n_rows, n_grp, per_peer, width)  9.06 us
  transfers between devices with their start and end apart: 7, of which 4 were waited for; matrix products, arithmetic and copies ran while one was open for 10% of the time, Pallas kernels for 0%

commit v1 on v0

--- a/solution.py
+++ b/solution.py
@@ -69,7 +69,8 @@
     spread = jnp.repeat(grad, hot_pick.shape[1], axis=0)
     hot_local = jax.ops.segment_sum(spread, hot_pick.reshape(-1), num_segments=hot_total)
     quarter = lax.psum_scatter(hot_local, "grp", scatter_dimension=0, tiled=True)
-    crossed = lax.psum(quarter, "rows")
+    pieces = lax.all_gather(quarter, "rows")
+    crossed = jnp.sum(pieces, axis=0)
     summed = lax.all_gather(crossed, "grp", axis=0, tiled=True)
     start = lax.axis_index(("rows", "grp")) * own_hot
     own_grad = lax.dynamic_slice_in_dim(summed, start, own_hot, 0)

time: 317 us -> 266 us (0.84)
  waiting for transfers between devices: 136 us -> 82.7 us
    psum x1 -> x0, waiting for transfers between devices: 72.4 us -> none  [body(): crossed = lax.psum(quarter, 'rows')]
    reduce_scatter x1, waiting for transfers between devices: 0.02 us -> 22.1 us  [body(): lax.psum_scatter(hot_local, 'grp', scatter_dimension=0, tiled=True)]
    all_to_all x1, waiting for transfers between devices: 36.3 us -> 14.7 us  [body(): lax.all_to_all(slot_grad.reshape(n_rows, n_grp, per_peer, width), 'rows',...]
    all_gather x0 -> x1, waiting for transfers between devices: none -> 19.2 us  [body(): pieces = lax.all_gather(quarter, 'rows')]
  transfers between devices with their start and end apart: 7 -> 7, of which waited for: 4 -> 5; matrix products, arithmetic and copies ran while one was open for 10% -> 13% of each run, Pallas kernels for 0% -> 0%
where the time goes in v1:
time: 266 us; the launch traced here: 265 us
  waiting for transfers between devices  82.7 us (31%)
  blocking collectives  68.2 us (26%)
  other arithmetic  39.8 us (15%)
  local copies, waits for them, and re-layouts  34 us (13%)
  starting transfers between devices  20.9 us (8%)
  between operations  14.3 us (5%)
  matrix products  4.82 us (2%)
    all_gather x1, blocking collectives, body(): lax.all_gather(table[hot_slot], ('rows', 'grp'), axis=0, tiled=True)  46.8 us
    all_to_all x1, waiting for transfers between devices, body(): lax.all_to_all(looked, 'rows', split_axis=0, concat_axis=0, tiled=True)  24.6 us
    reduce_scatter x1, waiting for transfers between devices, body(): lax.psum_scatter(hot_local, 'grp', scatter_dimension=0, tiled=True)  22.1 us
    all_gather x1, waiting for transfers between devices, body(): pieces = lax.all_gather(quarter, 'rows')  19.2 us
    all_to_all x1, waiting for transfers between devices, body(): lax.all_to_all(slot_grad.reshape(n_rows, n_grp, per_peer, width), 'rows',...  14.7 us
    all_to_all x1, blocking collectives, body(): lax.all_to_all(requests, 'rows', split_axis=0, concat_axis=0, tiled=True)  13.6 us
    scatter-add x1, other arithmetic, body(): jax.ops.segment_sum(delivered.reshape(slots, width), arrived.reshape(slot...  13.4 us
    scatter-add x1, other arithmetic, body(): jax.ops.segment_sum(spread, hot_pick.reshape(-1), num_segments=hot_total)  12.4 us
  transfers between devices with their start and end apart: 7, of which 5 were waited for; matrix products, arithmetic and copies ran while one was open for 13% of the time, Pallas kernels for 0%

profile of v1, /device:TPU:0, one launch (start us, length us, event | category | flops | bytes accessed | tf_op | source)
XLA Modules:
  0.0 264.7 jit_solution(10905864563783044367)
XLA Ops:
  8.0 13.6 %all_to_all.30 = s32[8,1,256]{2,1,0:T(1,128)S(1)} all-to-all(s32[8,1,256]{2,1,0:T(1,128)S(1)} %reshape.123), channel_id=1, replica_groups=mesh['rows'=8,'grp'=4] {'rows'}, dimensions={0} | all-to-all | bytes 16384 | tf_op jit(solution)/shard_map/all_to_all | solution.py:20
  23.5 3.2 %all-to-all-start.1 = ((s32[4,1,512]{2,1,0:T(1,128)}), s32[4,1,512]{2,1,0:T(1,128)S(1)}, u32[]{:S(2)}, u32[]{:S(2)}) async-start(s32[4,1,512]{2,1,0:T(1,128)} %reshape.125), calls=%async_computation.1 | async-start | bytes 16384 | tf_op jit(solution)/shard_map/all_to_all | solution.py:19
  28.5 2.1 all-to-all-done.1
  31.5 9.1 %gather_fusion = bf16[2048,256]{1,0:T(8,128)(2,1)} fusion(bf16[2048,256]{1,0:T(8,128)(2,1)S(1)} %convert_element_type.14, s32[2048]{0:T(1024)S(1)} %broadcast_clamp_fusion.1), kind=kCustom, calls=%fused_computation | custom fusion | bytes 2105344 | tf_op jit(solution)/shard_map/gather | solution.py:26
  40.5 4.4 %all-to-all-start.2 = ((bf16[8,4,64,256]{3,2,1,0:T(8,128)(2,1)}), bf16[8,4,64,256]{3,2,1,0:T(8,128)(2,1)}, u32[]{:S(2)}, u32[]{:S(2)}) async-start(bf16[8,4,64,256]{3,2,1,0:T(8,128)(2,1)} %bitcast.20), calls=%async_computation.2 | async-start | bytes 2097152 | tf_op jit(solution)/shard_map/all_to_all | solution.py:28
  46.4 24.6 %all-to-all-done.2 = bf16[8,4,64,256]{3,2,1,0:T(8,128)(2,1)} async-done(((bf16[8,4,64,256]{3,2,1,0:T(8,128)(2,1)}), bf16[8,4,64,256]{3,2,1,0:T(8,128)(2,1)}, u32[]{:S(2)}, u32[]{:S(2)}) %all-to-all-start.2) | async-done | bytes 1048608 | tf_op jit(solution)/shard_map/all_to_all | solution.py:28
  70.9 2.3 copy.49
  73.2 4.4 %all-to-all-start.3 = ((bf16[8,4,64,256]{3,2,0,1:T(8,128)(2,1)}), bf16[8,4,64,256]{3,2,0,1:T(8,128)(2,1)}, u32[]{:S(2)}, u32[]{:S(2)}) async-start(bf16[8,4,64,256]{3,2,0,1:T(8,128)(2,1)} %copy.49), calls=%async_computation.3 | async-start | bytes 2097152 | tf_op jit(solution)/shard_map/all_to_all | solution.py:27
  77.6 46.8 %all-gather = f32[512,256]{1,0:T(8,128)S(1)} all-gather(f32[16,256]{1,0:T(8,128)S(1)} %gather_fusion.1), channel_id=2, replica_groups=mesh['rows'=8,'grp'=4] {'rows','grp'}, dimensions={0}, use_global_device_ids=true | all-gather | bytes 540672 | tf_op jit(solution)/shard_map/all_gather | solution.py:16
  124.8 9.1 %gather_fusion.2 = bf16[2048,256]{1,0:T(8,128)(2,1)} fusion(bf16[512,256]{1,0:T(8,128)(2,1)S(1)} %convert_element_type.15, s32[2048]{0:T(1024)S(1)} %broadcast_clamp_fusion), kind=kCustom, calls=%fused_computation.2 | custom fusion | bytes 2105344 | tf_op jit(solution)/shard_map/gather | solution.py:40
  133.8 1.9 convert_reduce_fusion
  139.8 3.2 %fusion.2 = f32[2048,256]{1,0:T(8,128)} fusion(f32[256,256]{1,0:T(8,128)S(1)} %broadcast_multiply_fusion, s32[2048]{0:T(1024)S(1)} %eq.16), kind=kOutput, calls=%fused_computation.11 | convolution fusion | flops 1611137024 | bytes 2367488 | tf_op jit(solution)/shard_map/dot_general | solution.py:45
  142.9 4.3 %all-to-all-start.4 = ((f32[8,4,64,256]{3,2,1,0:T(8,128)}), f32[8,4,64,256]{3,2,1,0:T(8,128)}, u32[]{:S(2)}, u32[]{:S(2)}) async-start(f32[8,4,64,256]{3,2,1,0:T(8,128)} %bitcast.19), calls=%async_computation.4 | async-start | bytes 4194304 | tf_op jit(solution)/shard_map/all_to_all | solution.py:53
  147.6 12.4 %scatter_custom_fusion.1 = f32[512,256]{1,0:T(8,128)} fusion(s32[2048]{0:T(1024)S(1)} %reshape.94, f32[256,256]{1,0:T(8,128)S(1)} %broadcast_multiply_fusion, f32[]{:T(128)} %constant.15.clone.1), kind=kCustom, calls=%fused_computation.7 | custom fusion | flops 524288 | bytes 786436 | tf_op jit(solution)/shard_map/scatter-add | solution.py:70
  160.0 22.1 %reduce-scatter.2.cloned.1.call-done = f32[128,256]{1,0:T(8,128)} async-done(((f32[512,256]{1,0:T(8,128)}), f32[128,256]{1,0:T(8,128)}) %reduce-scatter.2.cloned.1.call-update) | async-done | bytes 131088 | tf_op jit(solution)/shard_map/reduce_scatter | solution.py:71
  182.2 14.7 %all-to-all-done.4 = f32[8,4,64,256]{3,2,1,0:T(8,128)} async-done(((f32[8,4,64,256]{3,2,1,0:T(8,128)}), f32[8,4,64,256]{3,2,1,0:T(8,128)}, u32[]{:S(2)}, u32[]{:S(2)}) %all-to-all-start.4) | async-done | bytes 2097184 | tf_op jit(solution)/shard_map/all_to_all | solution.py:53
  196.8 3.1 %copy.55 = f32[8,4,64,256]{3,2,0,1:T(8,128)} copy(f32[8,4,64,256]{3,2,1,0:T(8,128)} %all-to-all-done.4) | data formatting | bytes 4194304 | tf_op jit(solution)/shard_map/all_to_all | solution.py:53
  200.0 4.4 %all-to-all-start.5 = ((f32[8,4,64,256]{3,2,0,1:T(8,128)}), f32[8,4,64,256]{3,2,0,1:T(8,128)}, u32[]{:S(2)}, u32[]{:S(2)}) async-start(f32[8,4,64,256]{3,2,0,1:T(8,128)} %copy.55), calls=%async_computation.5 | async-start | bytes 4194304 | tf_op jit(solution)/shard_map/all_to_all | solution.py:52
  205.4 19.2 %all-gather.4.cloned.1.call-done = f32[1024,256]{1,0:T(8,128)} async-done(((f32[128,256]{1,0:T(8,128)}), f32[1024,256]{1,0:T(8,128)}) %all-gather.4.cloned.1.call-update) | async-done | bytes 1048592 | tf_op jit(solution)/shard_map/all_gather | solution.py:72
  225.9 7.8 %all_gather.15 = f32[512,256]{1,0:T(8,128)S(1)} all-gather(f32[128,256]{1,0:T(8,128)S(1)} %reduce_sum.29), channel_id=1, replica_groups=mesh['rows'=8,'grp'=4] {'grp'}, dimensions={0}, use_global_device_ids=true | all-gather | bytes 655360 | tf_op jit(solution)/shard_map/all_gather | solution.py:74
  234.6 3.1 %copy.56 = f32[8,4,64,256]{3,2,1,0:T(8,128)} copy(f32[8,4,64,256]{3,2,0,1:T(8,128)} %all-to-all-done.5) | data formatting | bytes 4194304 | tf_op jit(solution)/shard_map/all_to_all | solution.py:52
  237.7 13.4 %scatter_custom_fusion = f32[2048,256]{1,0:T(8,128)} fusion(s32[2048]{0:T(1024)S(1)} %reshape.86, f32[2048,256]{1,0:T(8,128)} %bitcast.21, f32[]{:T(128)} %constant.15.clone.1), kind=kCustom, calls=%fused_computation.15 | custom fusion | flops 524288 | bytes 2097664 | tf_op jit(solution)/shard_map/scatter-add | solution.py:65
  251.1 3.6 %scatter_custom_fusion.2 = f32[2048,256]{1,0:T(8,128)} fusion(f32[2048,256]{1,0:T(8,128)} %scatter_custom_fusion, s32[16]{0:T(128)S(1)} %compare_select_fusion.2, f32[512,256]{1,0:T(8,128)S(1)} %all_gather.15, s32[]{:T(128)S(6)} %select_n.23, s32[]{:T(128)} %constant.12.clone.1), kind=kCustom, calls=%fused_computation.25 | custom fusion | flops 4096 | bytes 2114052 | tf_op jit(solution)/shard_map/scatter-add | solution.py:77
  254.7 3.2 %multiply_subtract_fusion = f32[2048,256]{1,0:T(8,128)} fusion(f32[2048,256]{1,0:T(8,128)S(1)} %copy-done, f32[2048,256]{1,0:T(8,128)} %scatter_custom_fusion.2), kind=kLoop, calls=%fused_computation.9 | loop fusion | flops 1048576 | bytes 6291456 | tf_op jit(solution)/shard_map/sub | solution.py:78
  (54 shorter events, 14.5 us)
Async XLA Ops:
  23.5 7.0 %all-to-all-start.1 = ((s32[4,1,512]{2,1,0:T(1,128)}), s32[4,1,512]{2,1,0:T(1,128)S(1)}, u32[]{:S(2)}, u32[]{:S(2)}) async-start(s32[4,1,512]{2,1,0:T(1,128)} %reshape.125), calls=%async_computation.1 | async-start | bytes 16384 | tf_op jit(solution)/shard_map/all_to_all | solution.py:19
  31.5 13.5 %copy-start.1 = (f32[256,256]{1,0:T(8,128)S(1)}, f32[256,256]{1,0:T(8,128)}, u32[]{:S(2)}) copy-start(f32[256,256]{1,0:T(8,128)} %param.12) | copy-start | bytes 786436
  40.5 5.2 %copy-start.6 = (s32[16]{0:T(128)S(1)}, s32[16]{0:T(128)}, u32[]{:S(2)}) copy-start(s32[16]{0:T(128)} %param.8) | copy-start | bytes 196
  40.5 5.2 %copy-start = (f32[2048,256]{1,0:T(8,128)S(1)}, f32[2048,256]{1,0:T(8,128)}, u32[]{:S(2)}) copy-start(f32[2048,256]{1,0:T(8,128)} %param.7) | copy-start | bytes 6291460
  40.5 30.4 %all-to-all-start.2 = ((bf16[8,4,64,256]{3,2,1,0:T(8,128)(2,1)}), bf16[8,4,64,256]{3,2,1,0:T(8,128)(2,1)}, u32[]{:S(2)}, u32[]{:S(2)}) async-start(bf16[8,4,64,256]{3,2,1,0:T(8,128)(2,1)} %bitcast.20), calls=%async_computation.2 | async-start | bytes 2097152 | tf_op jit(solution)/shard_map/all_to_all | solution.py:28
  73.2 51.2 %copy-start.3 = (s32[256,8]{0,1:T(8,128)S(1)}, s32[256,8]{0,1:T(8,128)}, u32[]{:S(2)}) copy-start(s32[256,8]{0,1:T(8,128)} %param.11) | copy-start | bytes 24580
  73.2 63.4 %all-to-all-start.3 = ((bf16[8,4,64,256]{3,2,0,1:T(8,128)(2,1)}), bf16[8,4,64,256]{3,2,0,1:T(8,128)(2,1)}, u32[]{:S(2)}, u32[]{:S(2)}) async-start(bf16[8,4,64,256]{3,2,0,1:T(8,128)(2,1)} %copy.49), calls=%async_computation.3 | async-start | bytes 2097152 | tf_op jit(solution)/shard_map/all_to_all | solution.py:27
  124.7 11.8 %copy-start.4 = (s32[1,32,64]{2,1,0:T(8,128)S(1)}, s32[1,32,64]{2,1,0:T(8,128)}, u32[]{:S(2)}) copy-start(s32[1,32,64]{2,1,0:T(8,128)} %param.10) | copy-start | bytes 24580
  136.6 1.4 copy-start.2
  136.7 3.0 %copy-start.5 = (s32[256]{0:T(256)S(1)}, s32[256]{0:T(256)}, u32[]{:S(2)}) copy-start(s32[256]{0:T(256)} %param.13) | copy-start | bytes 3076
  142.9 53.9 %all-to-all-start.4 = ((f32[8,4,64,256]{3,2,1,0:T(8,128)}), f32[8,4,64,256]{3,2,1,0:T(8,128)}, u32[]{:S(2)}, u32[]{:S(2)}) async-start(f32[8,4,64,256]{3,2,1,0:T(8,128)} %bitcast.19), calls=%async_computation.4 | async-start | bytes 4194304 | tf_op jit(solution)/shard_map/all_to_all | solution.py:53
  147.3 34.9 %reduce-scatter.2.cloned.1.call-start = ((), (), s32[]{:S(2)}) async-start(), calls=%async_computation.7 | async-start | bytes 655360 | tf_op jit(solution)/shard_map/reduce_scatter | solution.py:71
  160.0 64.6 %all-gather.4.cloned.1.call-start = ((), (), s32[]{:S(2)}) async-start(), calls=%async_computation.8 | async-start | bytes 1179648 | tf_op jit(solution)/shard_map/all_gather | solution.py:72
  200.0 34.6 %all-to-all-start.5 = ((f32[8,4,64,256]{3,2,0,1:T(8,128)}), f32[8,4,64,256]{3,2,0,1:T(8,128)}, u32[]{:S(2)}, u32[]{:S(2)}) async-start(f32[8,4,64,256]{3,2,0,1:T(8,128)} %copy.55), calls=%async_computation.5 | async-start | bytes 4194304 | tf_op jit(solution)/shard_map/all_to_all | solution.py:52
Sparse Core Ops, SparseCore 0:
  160.1 21.9 reduce-scatter.1
  184.3 40.2 all-gather.3
